TPU v7x, 32 devices: a whole 2x2x4 slice. The times are simulated.
32 devices in a mesh: slab: 16 (over z, y, x), pencil: 2 (over core).
Axes of the slice: x: 2, y: 2, z: 4, core: 2. Of those that a mesh axis runs over, the one named last changes fastest.
Arguments:
- owner_map: int32 [16], replicated, may hold values from 0 to 15
- window_start: int32 [1], replicated, may hold values from 0 to 8
- child_maps: float32 [8, 20, 20], replicated, may hold values from -1 to 1
- innovation: float32 [20, 20], replicated, may hold values from -1.25 to 1.25
- coarse_bank: float32 [16, 20, 74898], P('slab'), may hold values from -6 to 6
- noise_middle: float32 [20, 64, 64, 128], P(None, 'slab', 'pencil'), may hold values from -6 to 6
- noise_finest: float32 [20, 128, 128, 256], P(None, 'slab', 'pencil'), may hold values from -6 to 6
Outputs:
- field_values: float32 [256, 256, 512], P('slab', 'pencil')
- zface_mean: float32 [128, 256, 512], P('slab', 'pencil')
- yface_mean: float32 [256, 128, 512], P('slab', 'pencil')
All inputs are finite; a program needn't handle non-finite values.
Results may differ from a plain program's by a relative error of at most 0.0001.
Values sent between devices are 32-bit elements; how exact they have to be, the bound alone decides.
No kernel may reach another device: no remote copies, remote signals or barrier semaphores. Data moves between devices by JAX's collectives and lax.ppermute only.
A program may use at most 448 MiB of HBM per device.

v0:
```python
import math

import jax
import jax.numpy as jnp
import numpy as np
from jax import lax
from jax.sharding import PartitionSpec as P

LEVELS = 8
ROOTS = 2
ROOTS_Z = 1
ROOTS_Y = 1


def from_root(block, axis, owner):
    block = jnp.where(lax.axis_index(axis) == owner, block, jnp.zeros_like(block))
    return lax.psum(block, axis)


def shifted(block, axis, distance):
    devices = range(lax.axis_size(axis))
    route = [((i - distance) % len(devices), i) for i in devices]
    return lax.ppermute(block, axis, route)


def legendre(order, point):
    values = [1.0, point, 1.5 * point * point - 0.5, 2.5 * point * point * point - 1.5 * point]
    return values[order]


def basis_table(points):
    table_rows = []
    for point in points:
        w_coord, v_coord, u_coord = point
        entry = []
        for deg_x in range(4):
            for deg_y in range(4):
                for deg_z in range(4):
                    if deg_x + deg_y + deg_z <= 3:
                        factor = math.sqrt((2 * deg_x + 1) * (2 * deg_y + 1) * (2 * deg_z + 1))
                        entry.append(
                            factor
                            * legendre(deg_x, u_coord)
                            * legendre(deg_y, v_coord)
                            * legendre(deg_z, w_coord)
                        )
        table_rows.append(entry)
    return jnp.asarray(np.array(table_rows), jnp.float32)


def level_span(level):
    first = ROOTS_Z * ROOTS_Y * ROOTS
    return (first * (8**level - 1) // 7, first * 8**level)


def level_block(flat, level):
    scale = 2**level
    offset, length = level_span(level)
    return flat[:, offset : offset + length].reshape(
        flat.shape[0], ROOTS_Z * scale, ROOTS_Y * scale, ROOTS * scale
    )


def descend(parent, child_maps):
    kids = jnp.einsum("okn,nzyx->okzyx", child_maps, parent, precision=lax.Precision.HIGHEST)
    count, planes, rows_y, cols_x = parent.shape
    kids = kids.reshape(2, 2, 2, count, planes, rows_y, cols_x).transpose(3, 4, 0, 5, 1, 6, 2)
    return kids.reshape(count, 2 * planes, 2 * rows_y, 2 * cols_x)


def innovate(innovation, noise):
    return jnp.einsum("kn,nzyx->kzyx", innovation, noise, precision=lax.Precision.HIGHEST)


def expand(table, coeffs):
    return jnp.einsum("pk,kzyx->pzyx", table, coeffs, precision=lax.Precision.HIGHEST)


def refine(coeffs, child_maps, plane_start, planes, row_start, rows):
    zero = jnp.zeros((), jnp.int32)
    plane_start = jnp.asarray(plane_start, jnp.int32)
    row_start = jnp.asarray(row_start, jnp.int32)
    parent_start = plane_start // 2
    parent_row = row_start // 2
    parent_planes = max(1, planes // 2)
    parent_rows = max(1, rows // 2)
    count = coeffs.shape[0]
    parents = lax.dynamic_slice(
        coeffs,
        (zero, parent_start, parent_row, zero),
        (count, parent_planes, parent_rows, coeffs.shape[3]),
    )
    spread = descend(parents, child_maps)
    return lax.dynamic_slice(
        spread,
        (zero, plane_start - 2 * parent_start, row_start - 2 * parent_row, zero),
        (count, planes, rows, spread.shape[3]),
    )


def shards(
    owner_map, window_start, child_maps, innovation, coarse_bank, noise_middle, noise_finest
):
    bank_levels = LEVELS - 2
    last_level = bank_levels - 1
    local_bank = coarse_bank[0]
    owners = [owner_map[window_start[0] + level] for level in range(bank_levels)]
    position = lax.axis_index("slab")
    coeffs = None
    received = [
        from_root(level_block(local_bank, level), "slab", owners[level])
        for level in range(last_level)
    ]
    for level in range(last_level):
        fresh = innovate(innovation, received[level])
        coeffs = fresh if level == 0 else descend(coeffs, child_maps) + fresh
    count, planes, rows_y, cols_x = noise_middle.shape
    first_plane = position * planes
    first_row = lax.axis_index("pencil") * rows_y
    top_start = first_plane // 2
    top_row = first_row // 2
    top_planes = max(1, planes // 2)
    top_rows = max(1, rows_y // 2)
    scale = 2**last_level
    bank_cols = ROOTS * scale
    zero = jnp.zeros((), jnp.int32)
    whole_bank = from_root(level_block(local_bank, last_level), "slab", owners[last_level])
    noise_top = lax.dynamic_slice(
        whole_bank, (zero, top_start, top_row, zero), (count, top_planes, top_rows, bank_cols)
    )
    upper_level = refine(coeffs, child_maps, top_start, top_planes, top_row, top_rows) + innovate(
        innovation, noise_top
    )
    middle = refine(
        upper_level,
        child_maps,
        first_plane - 2 * top_start,
        planes,
        first_row - 2 * top_row,
        rows_y,
    ) + innovate(innovation, noise_middle)
    fine = descend(middle, child_maps) + innovate(innovation, noise_finest)
    count, fine_planes, fine_rows, fine_cols = fine.shape
    halves = [-0.5, 0.5]
    inner = basis_table([(pz, py, px) for pz in halves for py in halves for px in halves])
    top = basis_table([(1.0, py, px) for py in halves for px in halves])
    bottom = basis_table([(-1.0, py, px) for py in halves for px in halves])
    north = basis_table([(pz, 1.0, px) for pz in halves for px in halves])
    south = basis_table([(pz, -1.0, px) for pz in halves for px in halves])
    values = (
        expand(inner, fine)
        .reshape(2, 2, 2, fine_planes, fine_rows, fine_cols)
        .transpose(3, 0, 4, 1, 5, 2)
    )
    field_values = values.reshape(2 * fine_planes, 2 * fine_rows, 2 * fine_cols)
    lower_faces = expand(bottom, fine)
    south_faces = expand(south, fine)
    above_coeffs = shifted(fine[:, :1], "slab", -1)
    beside_coeffs = shifted(fine[:, :, :1], "pencil", -1)
    above = expand(bottom, above_coeffs)
    beside = expand(south, beside_coeffs)
    lower_next = jnp.concatenate([lower_faces[:, 1:], above], axis=1)
    south_next = jnp.concatenate([south_faces[:, :, 1:], beside], axis=2)
    zsum = expand(top, fine) + lower_next
    zface = (0.5 * zsum).reshape(2, 2, fine_planes, fine_rows, fine_cols).transpose(2, 3, 0, 4, 1)
    zface_mean = zface.reshape(fine_planes, 2 * fine_rows, 2 * fine_cols)
    ysum = expand(north, fine) + south_next
    yface = (0.5 * ysum).reshape(2, 2, fine_planes, fine_rows, fine_cols).transpose(2, 0, 3, 4, 1)
    yface_mean = yface.reshape(2 * fine_planes, fine_rows, 2 * fine_cols)
    return (field_values, zface_mean, yface_mean)


def solution(mesh):
    placed = (
        P(),
        P(),
        P(),
        P(),
        P("slab", None, None),
        P(None, "slab", "pencil", None),
        P(None, "slab", "pencil", None),
    )
    return jax.shard_map(
        shards,
        mesh=mesh,
        in_specs=placed,
        out_specs=(P("slab", "pencil", None), P("slab", "pencil", None), P("slab", "pencil", None)),
        check_vma=False,
    )
```

profile of v0, /device:TPU:0, one launch (start us, length us, event | category | flops | bytes accessed | tf_op | source)
XLA Modules:
  0.0 1258.6 jit_solution(5010336957763130200)
XLA Ops:
  8.0 1.5 fusion.49
  11.5 26.7 %copy.91 = f32[1,20,74898]{1,2,0:T(8,128)} copy(f32[1,20,74898]{2,0,1:T(1,128)} %param.16) | data formatting | bytes 11983680 | tf_op args[4]
  38.2 1.9 slice_select_fusion.2
  40.1 4.6 slice_select_fusion.1
  44.7 22.8 %slice_select_fusion = f32[20,65536]{0,1:T(8,128)} fusion(f32[20,74898]{0,1:T(8,128)} %bitcast.227, pred[]{:T(512)S(6)} %eq.23), kind=kLoop, calls=%fused_computation | loop fusion | flops 1310720 | bytes 10485761 | tf_op jit(solution)/shard_map/jit(_where)/select_n | solution.py:16
  67.5 23.8 %copy.108 = f32[20,32,32,64]{3,0,2,1:T(8,128)} copy(f32[20,32,32,64]{0,3,2,1:T(8,128)} %bitcast.231) | data formatting | bytes 10485760 | tf_op jit(solution)/shard_map/jit(_where)/select_n | solution.py:16
  91.3 5.5 copy.103
  98.6 0.7 slice_select_fusion.5
  99.3 0.7 slice_select_fusion.4
  100.0 0.9 slice_select_fusion.3
  100.9 85.6 %all-reduce = (f32[20,2]{0,1:T(2,128)S(1)}, f32[20,2,2,4]{0,3,2,1:T(4,128)S(1)}, f32[20,4,4,8]{0,3,2,1:T(8,128)S(1)}) all-reduce(f32[20,2]{0,1:T(2,128)S(1)} %slice_select_fusion.5, f32[20,2,2,4]{0,3,2,1:T(4,128)S(1)} %bitcast.254, f32[20,4,4,8]{0,3,2,1:T(8,128)S(1)} %bitcast.252), channel_id=1, replica_groups=mesh['slab'=16,'pencil'=2] {'slab'}, use_global_device_ids=true, to_apply=%region_0.1 | all-reduce | flops 2920 | bytes 23360 | tf_op jit(solution)/shard_map/psum | solution.py:17
  186.7 0.6 convolution_bitcast_fusion.6
  187.5 0.6 fusion.35
  188.4 0.7 fusion.33
  189.3 3.2 fusion.12
  192.5 348.9 %all-reduce.4.cloned.1.call-done = (f32[20,8,8,16]{0,3,2,1:T(8,128)}, f32[20,16,16,32]{3,0,2,1:T(8,128)}, f32[20,32,32,64]{3,0,2,1:T(8,128)}) async-done(((f32[20,8,8,16]{0,3,2,1:T(8,128)}, f32[20,16,16,32]{3,0,2,1:T(8,128)}, f32[20,32,32,64]{3,0,2,1:T(8,128)}), (f32[20,8,8,16]{0,3,2,1:T(8,128)}, f32[20,16,16,32]{3,0,2,1:T(8,128)}, f32[20,32,32,64]{3,0,2,1:T(8,128)})) %all-reduce.4.cloned.1.call-update) | async-done | bytes 5980176 | tf_op jit(solution)/shard_map/psum | solution.py:17
  541.4 6.4 convolution_bitcast_fusion
  548.4 3.5 fusion.31
  551.9 2.9 copy.101
  554.9 1.7 convolution_bitcast_fusion.1
  556.6 0.7 copy.106
  557.7 1.5 fusion.18
  559.1 4.3 fusion.29
  563.4 12.3 copy.111
  575.7 5.2 copy.113
  581.0 13.9 %fusion.7 = f32[4,32,128,8,20]{2,4,3,1,0:T(8,128)} fusion(f32[20,4,32,128]{3,0,2,1:T(8,128)S(1)} %copy.113, f32[20,4,32,128]{3,0,2,1:T(8,128)} %fusion.12, f32[8,20,20,1,1]{2,0,1,4,3:T(8,128)S(1)} %bitcast.245), kind=kOutput, calls=%fused_computation.10 | convolution fusion | flops 629473280 | bytes 13120000 | tf_op jit(solution)/shard_map/okn,nzyx->okzyx/dot_general | solution.py:65
  594.8 78.5 %copy.115 = f32[2,2,2,20,4,32,128]{3,2,6,1,5,0,4:T(2,128)} copy(f32[2,2,2,20,4,32,128]{6,3,2,1,0,5,4:T(8,128)} %bitcast.233) | data formatting | bytes 20971520 | tf_op jit(solution)/shard_map/reshape | solution.py:67
  673.4 38.4 %copy.117 = f32[20,8,64,256]{3,0,2,1:T(8,128)} copy(f32[20,8,64,256]{0,3,2,1:T(8,128)} %bitcast.73) | data formatting | bytes 20971520 | tf_op jit(solution)/shard_map/reshape | solution.py:68
  711.8 23.1 %fusion.2 = f32[20,8,64,256]{3,0,2,1:T(8,128)S(1)} fusion(f32[20,8,64,256]{3,0,2,1:T(8,128)} %copy.117, f32[20,8,64,256]{3,2,1,0:T(8,128)} %param.18, f32[20,20]{1,0:T(8,128)S(1)} %copy-done.5), kind=kOutput, calls=%fused_computation.3 | convolution fusion | flops 631767040 | bytes 31458880 | tf_op jit(solution)/shard_map/kn,nzyx->kzyx/dot_general | solution.py:72
  735.0 0.7 slice.47
  735.9 1.5 copy.119
  737.3 3.2 collective-permute-start
  740.6 7.7 fusion.50
  748.3 86.5 %fusion.52 = f32[4,8,63,256]{3,0,2,1:T(4,128)} fusion(f32[4,20,1,1]{1,0,3,2:T(4,128)S(1)} %copy-done.12, f32[20,8,64,256]{3,0,2,1:T(8,128)S(1)} %fusion.2), kind=kOutput, calls=%fused_computation.67 | convolution fusion | flops 123863040 | bytes 12550464 | tf_op jit(solution)/shard_map/slice | solution.py:163
  834.8 16.2 %fusion.51 = f32[4,7,64,256]{3,0,2,1:T(4,128)} fusion(f32[4,20,1,1]{1,0,3,2:T(4,128)S(1)} %copy-done.7, f32[20,8,64,256]{3,0,2,1:T(8,128)S(1)} %fusion.2), kind=kOutput, calls=%fused_computation.66 | convolution fusion | flops 110100480 | bytes 12321088 | tf_op jit(solution)/shard_map/slice | solution.py:162
  850.9 5.8 reshape.129
  856.8 119.4 %copy.118 = f32[2,2,2,8,64,256]{2,5,1,4,0,3:T(8,128)} copy(f32[2,2,2,8,64,256]{5,2,1,0,4,3:T(2,128)} %reshape.129) | data formatting | bytes 8388608 | tf_op jit(solution)/shard_map/reshape | solution.py:152
  976.2 183.6 %reshape.130 = f32[16,128,512]{2,1,0:T(8,128)} reshape(f32[8,2,64,2,256,2]{5,4,3,2,1,0:T(8,128)} %bitcast.74) | data formatting | bytes 8388608 | tf_op jit(solution)/shard_map/reshape | solution.py:155
  1159.9 1.1 convolution_bitcast_fusion.5
  1161.0 10.3 fusion.6
  1171.3 2.9 reshape.135
  1174.3 4.4 copy.122
  1178.6 3.9 copy.124
  1182.6 2.9 fusion.19
  1185.5 9.6 fusion.5
  1195.1 2.6 reshape.132
  1197.7 33.7 %copy.121 = f32[2,2,8,64,256]{2,1,4,0,3:T(2,128)} copy(f32[2,2,8,64,256]{4,1,0,3,2:T(2,128)} %reshape.132) | data formatting | bytes 4194304 | tf_op jit(solution)/shard_map/reshape | solution.py:165
  1231.4 20.2 %copy.123 = f32[8,128,512]{2,1,0:T(8,128)} copy(f32[8,128,512]{0,2,1:T(8,128)} %bitcast.232) | data formatting | bytes 4194304
  (44 shorter events, 2.2 us)
Async XLA Ops:
  7.2 182.2 %copy-start = (f32[20,4,32,128]{3,2,1,0:T(8,128)S(1)}, f32[20,4,32,128]{3,2,1,0:T(8,128)}, u32[]{:S(2)}) copy-start(f32[20,4,32,128]{3,2,1,0:T(8,128)} %param.17) | copy-start | bytes 3932164
  7.2 534.3 %all-reduce.4.cloned.1.call-start = ((), (), s32[]{:S(2)}) async-start(), calls=%async_computation | async-start | bytes 32505856 | tf_op jit(solution)/shard_map/psum | solution.py:17
  96.8 89.8 %copy-start.5 = (f32[20,20]{1,0:T(8,128)S(1)}, f32[20,20]{1,0:T(8,128)}, u32[]{:S(2)}) copy-start(f32[20,20]{1,0:T(8,128)} %param.15) | copy-start | bytes 4804
  96.8 90.0 %copy-start.4 = (f32[8,20,20]{2,0,1:T(8,128)S(1)}, f32[8,20,20]{2,0,1:T(8,128)}, u32[]{:S(2)}) copy-start(f32[8,20,20]{2,0,1:T(8,128)} %param.14) | copy-start | bytes 38404
  541.4 6.4 copy-start.6
  734.9 99.8 %copy-start.2 = (f32[20,8,64,256]{3,0,2,1:T(8,128)}, f32[20,8,64,256]{3,0,2,1:T(8,128)S(1)}, u32[]{:S(2)}) copy-start(f32[20,8,64,256]{3,0,2,1:T(8,128)S(1)} %fusion.2) | copy-start | bytes 31457284
  735.0 5.6 copy-start.8
  735.8 424.1 %collective-permute-start.1 = (f32[20,8,1,256]{3,0,2,1:T(8,128)}, f32[20,8,1,256]{3,0,2,1:T(8,128)}, u32[]{:S(2)}, u32[]{:S(2)}) collective-permute-start(f32[20,8,1,256]{3,0,2,1:T(8,128)} %slice.47), channel_id=1, source_target_pairs={{1,0},{0,1},{3,2},{2,3},{5,4},{4,5},{7,6},{6,7},{9,8},{8,9},{11,10... | collective-permute-start | bytes 491528 | tf_op jit(solution)/shard_map/ppermute | solution.py:23
  737.3 11.0 copy-start.12
  737.3 445.2 %collective-permute-start = (f32[20,1,64,256]{3,2,1,0:T(8,128)}, f32[20,1,64,256]{3,2,1,0:T(8,128)}, u32[]{:S(2)}, u32[]{:S(2)}) collective-permute-start(f32[20,1,64,256]{3,2,1,0:T(8,128)} %copy.119), channel_id=1, source_target_pairs={{2,0},{4,2},{6,4},{8,6},{10,8},{12,10},{14,12},{16,14},{18,16},{20... | collective-permute-start | bytes 3932168 | tf_op jit(solution)/shard_map/ppermute | solution.py:23
  748.3 86.5 %copy-start.7 = (f32[4,20,1,1]{1,0,3,2:T(4,128)S(1)}, f32[4,20,1,1]{1,0,3,2:T(4,128)}, u32[]{:S(2)}) copy-start(f32[4,20,1,1]{1,0,3,2:T(4,128)} %constant.107) | copy-start | bytes 964
  976.2 183.6 %copy-start.11 = (f32[4,20,1]{1,0,2:T(4,128)S(1)}, f32[4,20,1]{1,0,2:T(4,128)}, u32[]{:S(2)}) copy-start(f32[4,20,1]{1,0,2:T(4,128)} %constant.111) | copy-start | bytes 964
  976.2 184.8 %copy-start.3 = (f32[4,8,63,256]{3,0,2,1:T(4,128)S(1)}, f32[4,8,63,256]{3,0,2,1:T(4,128)}, u32[]{:S(2)}) copy-start(f32[4,8,63,256]{3,0,2,1:T(4,128)} %fusion.52) | copy-start | bytes 6193156
  976.2 184.8 %copy-start.10 = (f32[4,20,1,1]{1,0,3,2:T(4,128)S(1)}, f32[4,20,1,1]{1,0,3,2:T(4,128)}, u32[]{:S(2)}) copy-start(f32[4,20,1,1]{1,0,3,2:T(4,128)} %constant.109) | copy-start | bytes 964
  1178.6 3.9 copy-start.13
  1178.6 6.9 copy-start.9
  1231.4 20.2 %copy-start.1 = (f32[20,4,32,128]{3,2,1,0:T(8,128)S(1)}, f32[20,4,32,128]{3,2,1,0:T(8,128)}, u32[]{:S(2)}) copy-start(f32[20,4,32,128]{3,2,1,0:T(8,128)} %param.17) | copy-start | bytes 3932164
Sparse Core Ops, SparseCore 0:
  96.9 444.4 all-reduce.3
where the time goes:
time: 1280 us; the launch traced here: 1260 us
  local copies, waits for them, and re-layouts  575 us (45%)
  waiting for transfers between devices  349 us (27%)
  matrix products  195 us (15%)
  blocking collectives  85.6 us (7%)
  other arithmetic  31.6 us (2%)
  between operations  19.1 us (1%)
    psum x1, waiting for transfers between devices, from_root(): return lax.psum(block, axis)  349 us
    reshape x1, local copies, waits for them, and re-layouts, shards(): field_values = values.reshape(2 * fine_planes, 2 * fine_rows, 2 * fine_cols)  184 us
    reshape x2, local copies, waits for them, and re-layouts, shards(): values = expand(inner, fine).reshape(2, 2, 2, fine_planes, fine_rows, fin...  125 us
    reshape x3, local copies, waits for them, and re-layouts, descend(): kids.reshape(2, 2, 2, count, planes, rows_y, cols_x)  93.8 us
    slice x1, matrix products, shards(): south_next = jnp.concatenate([south_faces[:, :, 1:], beside], axis=2)  86.5 us
    psum x1, blocking collectives, from_root(): return lax.psum(block, axis)  85.6 us
    unnamed x32, local copies, waits for them, and re-layouts  51 us
    reshape x3, local copies, waits for them, and re-layouts, descend(): return kids.reshape(count, 2 * planes, 2 * rows_y, 2 * cols_x)  44.1 us
  transfers between devices with their start and end apart: 3, of which 1 were waited for; matrix products, arithmetic and copies ran while one was open for 36% of the time, Pallas kernels for 0%

commit v1 on v0

v1 whole, which is shorter than its diff:
```python
import math

import jax
import jax.numpy as jnp
import numpy as np
from jax import lax
from jax.experimental import pallas as pl
from jax.experimental.pallas import tpu as pltpu
from jax.sharding import PartitionSpec as P

LEVELS = 8
ROOTS = 2
BANK = LEVELS - 2
LANES = 128
SUB = 8
HIGH = lax.Precision.HIGHEST


def legendre(order, point):
    values = [1.0, point, 1.5 * point * point - 0.5, 2.5 * point * point * point - 1.5 * point]
    return values[order]


def basis_row(pz, py, px):
    entry = []
    for deg_x in range(4):
        for deg_y in range(4):
            for deg_z in range(4):
                if deg_x + deg_y + deg_z <= 3:
                    factor = math.sqrt((2 * deg_x + 1) * (2 * deg_y + 1) * (2 * deg_z + 1))
                    entry.append(
                        factor * legendre(deg_x, px) * legendre(deg_y, py) * legendre(deg_z, pz)
                    )
    return entry


def fine_layout():
    halves = [-0.5, 0.5]
    table, index = [], {}

    def functional(key, row):
        if key not in index:
            index[key] = len(table)
            table.append(row)
        return index[key]

    rows = []
    for px in halves:
        for pz in halves:
            for y2 in range(2 * SUB):
                py = halves[y2 % 2]
                rows.append([(y2 // 2, functional((pz, py, px), basis_row(pz, py, px)))])
        for w in (1.0, -1.0):
            for y2 in range(2 * SUB):
                py = halves[y2 % 2]
                half_row = [0.5 * v for v in basis_row(w, py, px)]
                rows.append([(y2 // 2, functional((w, py, px), half_row))])
        for pz in halves:
            north = functional((pz, 1.0, px), [0.5 * v for v in basis_row(pz, 1.0, px)])
            south = functional((pz, -1.0, px), [0.5 * v for v in basis_row(pz, -1.0, px)])
            for y in range(SUB):
                row = [(y, north)]
                if y + 1 < SUB:
                    row.append((y + 1, south))
                rows.append(row)
        for pz in halves:
            south = functional((pz, -1.0, px), [0.5 * v for v in basis_row(pz, -1.0, px)])
            for y in range(SUB):
                rows.append([(0, south)] if y == SUB - 1 else [])
    return np.array(table, np.float32), rows


def selector(rows, functionals):
    chosen = np.zeros((len(rows), SUB, functionals), np.float32)
    for r, terms in enumerate(rows):
        for y, f in terms:
            chosen[r, y, f] = 1.0
    return chosen


def left_factors(maps, chosen):
    m, _, f = chosen.shape
    k = maps.shape[2]
    own = jnp.einsum("ryf,fn->rny", chosen, maps[0], precision=HIGH).reshape(1, m, k * SUB)
    pairs = chosen.reshape(m, SUB // 2, 2, f)
    octants = maps[1:].reshape(2, 2, 2, f, k)
    par = jnp.einsum("rqyf,zyxfn->zrnxq", pairs, octants, precision=HIGH).reshape(2, m, k * SUB)
    return jnp.concatenate([own, par], axis=0)


class Plan:
    def __init__(self, mid_planes, mid_rows, slabs, pencils):
        self.slabs, self.pencils = slabs, pencils
        self.mid_planes, self.mid_rows = mid_planes, mid_rows
        self.w, self.r, self.x, self.n, self.off, self.place = [], [], [], [], [], []
        for j in range(BANK):
            self.w.append(max(1, mid_planes >> (BANK - j)))
            self.r.append(max(1, mid_rows >> (BANK - j)))
            self.x.append(ROOTS << j)
            self.n.append(self.w[j] * self.r[j] * self.x[j])
            self.off.append(ROOTS * (8**j - 1) // 7)
        self.big = [j for j in range(BANK) if self.r[j] * self.x[j] % LANES == 0]
        self.small = [j for j in range(BANK) if j not in self.big]
        lane = 0
        self.place = [0] * BANK
        for j in reversed(self.big):
            self.place[j] = lane
            lane += self.n[j]
        self.small_at = lane
        for j in reversed(self.small):
            assert self.w[j] == 1
            self.place[j] = lane
            lane += self.n[j]
        assert lane - self.small_at <= LANES
        self.chunks = (self.small_at + LANES) // LANES

    def z0(self, j, slab):
        return (slab * self.mid_planes) >> (BANK - j)

    def y0(self, j, pencil):
        return (pencil * self.mid_rows) >> (BANK - j)


def pack_kernel(plan, where_ref, bank_ref, out_ref):
    slab = pl.program_id(0)
    pencil = where_ref[0]
    k = bank_ref.shape[1]

    def put(chunk, value):
        out_ref[0, chunk * k : (chunk + 1) * k, :] = value

    for j in plan.big:
        rows = 2**j
        length = plan.r[j] * plan.x[j]
        base = plan.off[j] // LANES * LANES
        delta = plan.off[j] - base
        for plane in range(plan.w[j]):
            start = (plan.z0(j, slab) + plane) * rows * plan.x[j] + plan.y0(j, pencil) * plan.x[j]
            start = pl.multiple_of(base + start, LANES)
            wide = bank_ref[0, :, pl.ds(start, length + LANES)]
            if delta:
                wide = pltpu.roll(wide, length + LANES - delta, 1)
            at = (plan.place[j] + plane * length) // LANES
            for c in range(length // LANES):
                put(at + c, wide[:, c * LANES : (c + 1) * LANES])
    lane = lax.broadcasted_iota(jnp.int32, (k, LANES), 1)
    small = jnp.zeros((k, LANES), jnp.float32)
    for j in plan.small:
        base = plan.off[j] // LANES * LANES
        end = -(-(plan.off[j] + ROOTS * 8**j) // LANES) * LANES
        size = end - base
        start = plan.off[j] - base
        start = start + (plan.z0(j, slab) * 2**j + plan.y0(j, pencil)) * plan.x[j]
        at = plan.place[j] - plan.small_at
        shift = lax.rem(at - start + 2 * size, size)
        moved = pltpu.roll(bank_ref[0, :, base:end], shift, 1)[:, :LANES]
        small = jnp.where((lane >= at) & (lane < at + plan.n[j]), moved, small)
    put(plan.small_at // LANES, small)


def split3(value):
    hi = value.astype(jnp.bfloat16)
    rest = value - hi.astype(jnp.float32)
    mid = rest.astype(jnp.bfloat16)
    lo = (rest - mid.astype(jnp.float32)).astype(jnp.bfloat16)
    return hi, mid, lo


def split2(value):
    hi = value.astype(jnp.bfloat16)
    lo = (value - hi.astype(jnp.float32)).astype(jnp.bfloat16)
    return hi, lo


def dot(left, right):
    return lax.dot_general(
        left, right, (((1,), (0,)), ((), ())), preferred_element_type=jnp.float32
    )


def coarse_kernel(plan, k, ints_ref, recv_ref, left_ref, out_ref):
    kp = 24
    lh, ll = split2(left_ref[...])
    left = jnp.concatenate([lh, lh, ll], axis=1)

    def chunk_of(j, c):
        return recv_ref[ints_ref[j], c * k : (c + 1) * k, :]

    coeffs = None
    for j in range(BANK):
        n = max(LANES, plan.n[j])
        if j in plan.small:
            at = plan.place[j] - plan.small_at
            noise = chunk_of(j, plan.small_at // LANES)
            if at:
                noise = pltpu.roll(noise, LANES - at, 1)
        else:
            first = plan.place[j] // LANES
            noise = jnp.concatenate([chunk_of(j, first + c) for c in range(n // LANES)], axis=1)
        noise = jnp.concatenate([noise, jnp.zeros((kp - k, n), jnp.float32)], axis=0)
        pieces = []
        if j == 0:
            pieces = [jnp.zeros((8 * kp, n), jnp.float32)]
        else:
            lane = lax.broadcasted_iota(jnp.int32, (1, n), 1)
            x = lane & (plan.x[j] - 1)
            row = (lane // plan.x[j]) & (plan.r[j] - 1)
            plane = lane // (plan.x[j] * plan.r[j])
            y_odd = (row & 1) if plan.r[j] > 1 else ints_ref[2 * BANK + j]
            z_odd = (plane & 1) if plan.w[j] > 1 else ints_ref[BANK + j]
            octant = 4 * z_odd + 2 * y_odd + (x & 1)
            parent = ((plane // 2) * plan.r[j - 1] + row // 2) * plan.x[j - 1] + x // 2
            parents = coeffs.shape[1]
            spot = lax.broadcasted_iota(jnp.int32, (parents, n), 0)
            onehot = jnp.where(spot == parent, 1.0, 0.0).astype(jnp.bfloat16)
            parts = jnp.concatenate([p.astype(jnp.float32) for p in split3(coeffs)], axis=0)
            up = dot(parts.astype(jnp.bfloat16), onehot)
            up = up[:kp] + up[kp : 2 * kp] + up[2 * kp :]
            pieces = [jnp.where(octant == o, up, 0.0) for o in range(8)]
        right = jnp.concatenate(pieces + [noise], axis=0)
        rh, rl = split2(right)
        coeffs = dot(left, jnp.concatenate([rh, rl, rh], axis=0))
    out_ref[...] = coeffs


def lift(block, sources, half):
    k = block.shape[0]
    flat = block.reshape(k * SUB, LANES)
    lane = lax.broadcasted_iota(jnp.int32, (k * SUB, LANES), 1)
    row = lax.broadcasted_iota(jnp.int32, (k, SUB, LANES), 1)
    even = (lax.broadcasted_iota(jnp.int32, (k, SUB, LANES), 2) & 1) == 0
    low = row < SUB // 2
    wide = []
    for c in range(sources):
        up = jnp.take_along_axis(
            flat, lane // 2 + c * (LANES // 2), axis=1, mode="promise_in_bounds"
        ).reshape(k, SUB, LANES)
        turned = pltpu.roll(up, SUB // 2, 1)
        both = jnp.where(low, up, turned) if half == 0 else jnp.where(low, turned, up)
        wide.append(jnp.where(low == even, both, 0.0).reshape(k * SUB, LANES))
    return jnp.concatenate(wide, axis=1) if sources > 1 else wide[0]


def operand(noise, raised):
    nh, nl = split2(noise)
    ph, pl_ = split2(raised)
    return jnp.concatenate([nh, nl, nh, ph, pl_, ph], axis=0)


def fine_kernel(
    ints_ref, mid_left, fine_left, upper, noise_mid, noise, field, zface, yface, zfirst, sfirst,
    mid, mid_s, fine_s, zcarry,
):
    step = pl.program_id(0)
    steps = pl.num_programs(0)
    plane = steps - 1 - step
    k = noise.shape[0]
    rows, cols = noise.shape[2], noise.shape[3]
    mid_planes, mid_rows, mid_cols = noise_mid.shape[1:]

    @pl.when(step == 0)
    def _():
        for source, target in ((mid_left, mid_s), (fine_left, fine_s)):
            wh, wl = split2(source[0])
            for oz in range(2):
                vh, vl = split2(source[1 + oz])
                target[oz] = jnp.concatenate([wh, wh, wl, vh, vh, vl], axis=1)
        for z in range(mid_planes):
            left = mid_s[(ints_ref[0] + z) % 2]
            for yb in range(mid_rows // 16):
                parent = upper[:, z // 2, yb * SUB : (yb + 1) * SUB, :]
                for half in range(2):
                    y = yb * 16 + half * SUB
                    own = noise_mid[:, z, y : y + SUB, :].reshape(k * SUB, mid_cols)
                    got = dot(left, operand(own, lift(parent, 1, half)))
                    mid[:, z, y : y + SUB, :] = got.reshape(k, SUB, mid_cols)
        zcarry[...] = jnp.zeros(zcarry.shape, jnp.float32)

    left = fine_s[plane % 2]
    group = left.shape[0] // 2
    sources = cols // LANES
    lane = lax.broadcasted_iota(jnp.int32, (group, LANES), 1)
    even = (lane & 1) == 0
    south = [jnp.zeros((2 * SUB, LANES), jnp.float32) for _ in range(2 * sources)]
    for yb in reversed(range(rows // 16)):
        parent = mid[:, plane // 2, yb * SUB : (yb + 1) * SUB, :]
        for half in (1, 0):
            y = yb * 16 + half * SUB
            own = noise[:, 0, y : y + SUB, :].reshape(k * SUB, cols)
            got = dot(left, operand(own, lift(parent, sources, half)))
            for c in range(2 * sources):
                s = c // 2
                index = lane // 2 + (c % 2) * (LANES // 2)
                span = slice(s * LANES, (s + 1) * LANES)
                a = jnp.take_along_axis(
                    got[:group, span], index, axis=1, mode="promise_in_bounds"
                )
                b = jnp.take_along_axis(
                    got[group:, span], index, axis=1, mode="promise_in_bounds"
                )
                out = jnp.where(even, a, b)
                to = slice(c * LANES, (c + 1) * LANES)
                y2 = slice(2 * y, 2 * y + 16)
                field[0, y2, to] = out[0:16]
                field[1, y2, to] = out[16:32]
                zface[0, y2, to] = out[32:48] + zcarry[y2, to]
                zcarry[y2, to] = out[48:64]
                faces = out[64:80] + south[c]
                yface[0, y : y + SUB, to] = faces[:SUB]
                yface[1, y : y + SUB, to] = faces[SUB:]
                south[c] = out[80:96]
    for c in range(2 * sources):
        to = slice(c * LANES, (c + 1) * LANES)
        sfirst[0, :, to] = south[c]

    @pl.when(plane == 0)
    def _():
        zfirst[...] = zcarry[...]


def shards(
    owner_map, window_start, child_maps, innovation, coarse_bank, noise_middle, noise_finest
):
    slabs, pencils = lax.axis_size("slab"), lax.axis_size("pencil")
    slab, pencil = lax.axis_index("slab"), lax.axis_index("pencil")
    k, mid_planes, mid_rows, mid_cols = noise_middle.shape
    _, planes, rows, cols = noise_finest.shape
    plan = Plan(mid_planes, mid_rows, slabs, pencils)
    f32 = jnp.float32
    smem = pl.BlockSpec(memory_space=pltpu.SMEM)

    def whole(shape):
        return pl.BlockSpec(shape, lambda *_: (0,) * len(shape))

    packed_rows = plan.chunks * k
    packed = pl.pallas_call(
        lambda *refs: pack_kernel(plan, *refs),
        grid=(slabs,),
        in_specs=[smem, whole((1, k, -(-coarse_bank.shape[2] // LANES) * LANES))],
        out_specs=pl.BlockSpec((1, packed_rows, LANES), lambda s: (s, 0, 0)),
        out_shape=jax.ShapeDtypeStruct((slabs, packed_rows, LANES), f32),
        compiler_params=pltpu.CompilerParams(vmem_limit_bytes=48 << 20),
        name="pack",
    )(pencil.reshape(1).astype(jnp.int32), coarse_bank)
    recv = lax.all_to_all(packed, "slab", 0, 0, tiled=True)

    table, fine_rows = fine_layout()
    maps = jnp.concatenate([innovation[None], child_maps], axis=0)
    fine_maps = jnp.einsum("fk,mkn->mfn", jnp.asarray(table), maps, precision=HIGH)
    fine_left = left_factors(fine_maps, selector(fine_rows, table.shape[0]))
    mid_left = left_factors(maps, selector([[(y, o)] for o in range(k) for y in range(SUB)], k))
    owners = lax.dynamic_slice(owner_map, (window_start[0],), (BANK,))
    z_odd = jnp.stack([plan.z0(j, slab) % 2 for j in range(BANK)])
    y_odd = jnp.stack([plan.y0(j, pencil) % 2 for j in range(BANK)])
    ints = jnp.concatenate([owners, z_odd, y_odd]).astype(jnp.int32)
    coarse_left = jnp.concatenate([child_maps, innovation[None]], axis=0)
    coarse_left = jnp.pad(coarse_left, ((0, 0), (0, 24 - k), (0, 24 - k)))
    coarse_left = coarse_left.transpose(1, 0, 2).reshape(24, 9 * 24)

    last = BANK - 1
    upper = pl.pallas_call(
        lambda *refs: coarse_kernel(plan, k, *refs),
        in_specs=[smem, pl.BlockSpec(memory_space=pltpu.VMEM), pl.BlockSpec(memory_space=pltpu.VMEM)],
        out_specs=pl.BlockSpec(memory_space=pltpu.VMEM),
        out_shape=jax.ShapeDtypeStruct((24, plan.n[last]), f32),
        compiler_params=pltpu.CompilerParams(vmem_limit_bytes=48 << 20),
        name="coarse",
    )(ints, recv, coarse_left)
    upper = upper[:k].reshape(k, plan.w[last], plan.r[last], plan.x[last])
    upper = jnp.pad(upper, ((0, 0), (0, 0), (0, 0), (0, LANES - plan.x[last])))

    m_fine = fine_left.shape[1]
    depth = 6 * k * SUB
    flip = planes - 1
    field, zface, yface, zfirst, sfirst = pl.pallas_call(
        fine_kernel,
        grid=(planes,),
        in_specs=[
            smem,
            whole(mid_left.shape),
            whole(fine_left.shape),
            whole(upper.shape),
            whole(noise_middle.shape),
            pl.BlockSpec((k, 1, rows, cols), lambda i: (0, flip - i, 0, 0)),
        ],
        out_specs=[
            pl.BlockSpec((2, 2 * rows, 2 * cols), lambda i: (flip - i, 0, 0)),
            pl.BlockSpec((1, 2 * rows, 2 * cols), lambda i: (flip - i, 0, 0)),
            pl.BlockSpec((2, rows, 2 * cols), lambda i: (flip - i, 0, 0)),
            whole((2 * rows, 2 * cols)),
            pl.BlockSpec((1, 2 * SUB, 2 * cols), lambda i: (flip - i, 0, 0)),
        ],
        out_shape=[
            jax.ShapeDtypeStruct((2 * planes, 2 * rows, 2 * cols), f32),
            jax.ShapeDtypeStruct((planes, 2 * rows, 2 * cols), f32),
            jax.ShapeDtypeStruct((2 * planes, rows, 2 * cols), f32),
            jax.ShapeDtypeStruct((2 * rows, 2 * cols), f32),
            jax.ShapeDtypeStruct((planes, 2 * SUB, 2 * cols), f32),
        ],
        scratch_shapes=[
            pltpu.VMEM((k, mid_planes, mid_rows, mid_cols), f32),
            pltpu.VMEM((2, mid_left.shape[1], depth), jnp.bfloat16),
            pltpu.VMEM((2, m_fine, depth), jnp.bfloat16),
            pltpu.VMEM((2 * rows, 2 * cols), f32),
        ],
        compiler_params=pltpu.CompilerParams(
            dimension_semantics=("arbitrary",), vmem_limit_bytes=52 << 20
        ),
        name="fine",
    )(
        (slab * mid_planes % 2).reshape(1).astype(jnp.int32),
        mid_left, fine_left, upper, noise_middle, noise_finest,
    )

    above = lax.ppermute(zfirst, "slab", [((i + 1) % slabs, i) for i in range(slabs)])
    edge = sfirst.reshape(2 * planes, SUB, 2 * cols)[:, SUB - 1]
    beside = lax.ppermute(edge, "pencil", [((i + 1) % pencils, i) for i in range(pencils)])
    zface = zface.at[planes - 1].add(above)
    yface = yface.at[:, rows - 1].add(beside)
    return (field, zface, yface)


def solution(mesh):
    placed = (
        P(),
        P(),
        P(),
        P(),
        P("slab", None, None),
        P(None, "slab", "pencil", None),
        P(None, "slab", "pencil", None),
    )
    return jax.shard_map(
        shards,
        mesh=mesh,
        in_specs=placed,
        out_specs=(P("slab", "pencil", None), P("slab", "pencil", None), P("slab", "pencil", None)),
        check_vma=False,
    )
```

time: 1280 us -> 134 us (0.10); the launches traced: 1260 us -> 134 us
  local copies, waits for them, and re-layouts: 575 us -> 18.7 us
  waiting for transfers between devices: 349 us -> 46.4 us
  matrix products: 195 us -> 6.51 us
  blocking collectives: 85.6 us -> 0 us
  Pallas kernels: 0 us -> 31.9 us
  other arithmetic: 31.6 us -> 6.39 us
  starting transfers between devices: 3.32 us -> 22.3 us
  between operations: 19.1 us -> 1.54 us
    reshape x13 -> x7, local copies, waits for them, and re-layouts: 490 us -> 4.62 us  [the longest x2 1.85 us: left_factors(): jnp.einsum('rqyf,zyxfn->zrnxq', pairs, octants, precision=HIGH)]
    psum x1 -> x0, waiting for transfers between devices: 349 us -> none  [from_root(): return lax.psum(block, axis)]
    slice x2 -> x0, matrix products: 103 us -> none  [the longest x1 86.5 us: shards(): south_next = jnp.concatenate([south_faces[:, :, 1:], beside], axis=2)]
    psum x1 -> x0, blocking collectives: 85.6 us -> none  [from_root(): return lax.psum(block, axis)]
    dot_general x20 -> x5, matrix products: 92 us -> 6.51 us  [the longest x2 2.87 us: left_factors(): jnp.einsum('rqyf,zyxfn->zrnxq', pairs, octants, precision=HIGH)]
    all_to_all x0 -> x1, waiting for transfers between devices: none -> 43 us  [shards(): recv = lax.all_to_all(packed, 'slab', 0, 0, tiled=True)]
    unnamed x32 -> x24, local copies, waits for them, and re-layouts: 51 us -> 11.3 us
    pallas_call x0 -> x3, Pallas kernels: none -> 31.9 us  [the longest x1 23 us: shards(): pl.pallas_call(fine_kernel, grid=(planes,), in_specs=[smem, whole(mid_lef...]
  transfers between devices with their start and end apart: 3 -> 3, of which waited for: 1 -> 2; matrix products, arithmetic and copies ran while one was open for 36% -> 14% of each run, Pallas kernels for 0% -> 0%
where the time goes in v1:
time: 134 us
  waiting for transfers between devices  46.4 us (35%)
  Pallas kernels  31.9 us (24%)
  starting transfers between devices  22.3 us (17%)
  local copies, waits for them, and re-layouts  18.7 us (14%)
  matrix products  6.51 us (5%)
  other arithmetic  6.39 us (5%)
  between operations  1.54 us (1%)
    all_to_all x1, waiting for transfers between devices, shards(): recv = lax.all_to_all(packed, 'slab', 0, 0, tiled=True)  43 us
    pallas_call x1, Pallas kernels, shards(): pl.pallas_call(fine_kernel, grid=(planes,), in_specs=[smem, whole(mid_lef...  23 us
    ppermute x1, starting transfers between devices, shards(): lax.ppermute(zfirst, 'slab', [((i + 1) % slabs, i) for i in range(slabs)])  13.8 us
    unnamed x24, local copies, waits for them, and re-layouts  11.3 us
    all_to_all x1, starting transfers between devices, shards(): recv = lax.all_to_all(packed, 'slab', 0, 0, tiled=True)  8.47 us
    pallas_call x1, Pallas kernels, shards(): pl.pallas_call(lambda *refs: pack_kernel(plan, *refs), grid=(slabs,), in_...  6.11 us
    concatenate x2, other arithmetic, left_factors(): return jnp.concatenate([own, par], axis=0)  3.68 us
    ppermute x1, waiting for transfers between devices, shards(): lax.ppermute(zfirst, 'slab', [((i + 1) % slabs, i) for i in range(slabs)])  3.41 us
  transfers between devices with their start and end apart: 3, of which 2 were waited for; matrix products, arithmetic and copies ran while one was open for 14% of the time, Pallas kernels for 0%

profile of v1, /device:TPU:0, one launch (start us, length us, event | category | flops | bytes accessed | tf_op | source)
XLA Modules:
  0.0 133.7 jit_solution(2391872051343348711)
XLA Ops:
  0.6 6.2 %copy.40.refs_1_ = f32[1,20,74898]{2,1,0:T(8,128)} copy(f32[1,20,74898]{2,0,1:T(1,128)} %param.20) | data formatting | bytes 11983680 | tf_op args[4]
  6.8 6.1 %pack.1 = f32[16,380,128]{2,1,0:T(8,128)S(1)} custom-call(s32[1]{0:T(128)} %bitcast.40.refs_0_, f32[1,20,74898]{2,1,0:T(8,128)} %copy.40.refs_1_), custom_call_target="tpu_custom_call" | custom-call | tf_op jit(solution)/shard_map/pack/pallas_call | solution.py:336
  12.9 0.0 copy-start
  12.9 1.7 %copy-done = f32[16,380,128]{2,1,0:T(8,128)} copy-done((f32[16,380,128]{2,1,0:T(8,128)}, f32[16,380,128]{2,1,0:T(8,128)S(1)}, u32[]{:S(2)}) %copy-start) | copy-done | bytes 3112984
  14.6 8.5 %all-to-all-start = ((f32[16,380,128]{2,1,0:T(8,128)}), f32[16,380,128]{2,1,0:T(8,128)S(1)}, u32[]{:S(2)}, u32[]{:S(2)}) async-start(f32[16,380,128]{2,1,0:T(8,128)} %copy-done), calls=%async_computation | async-start | bytes 6291456 | tf_op jit(solution)/shard_map/all_to_all | solution.py:345
  23.8 0.0 copy-done.7
  23.8 0.1 copy.33
  23.9 0.1 copy.41
  24.0 0.5 copy-done.6
  24.5 0.1 copy.34
  24.6 0.1 copy.42
  24.8 0.1 copy.43.refs_2_
  24.8 1.1 convolution_bitcast_fusion.4
  25.9 0.0 copy-start.5
  25.9 0.6 copy-done.5
  26.5 1.4 %convolution_bitcast_fusion = f32[2,192,20,2,4]{1,2,4,3,0:T(8,128)S(1)} fusion(f32[192,4,2,24,1,1]{0,3,2,1,5,4:T(8,128)} %constant.165, f32[2,2,2,24,20,1]{3,4,2,1,0,5:T(8,128)S(1)} %bitcast.89), kind=kOutput, calls=%fused_computation | convolution fusion | flops 35389440 | bytes 408576 | tf_op jit(solution)/shard_map/rqyf,zyxfn->zrnxq/dot_general | solution.py:87
  28.0 0.3 copy.37
  28.2 0.0 copy-start.8
  28.3 0.9 copy.39
  29.2 1.2 convolution_bitcast_fusion.2
  30.4 0.0 copy-start.9
  30.5 0.1 copy.60
  30.5 0.8 copy.38
  31.3 1.0 copy.29
  32.3 1.4 %convolution_bitcast_fusion.1 = f32[2,160,20,2,4]{1,2,3,0,4:T(8,128)S(1)} fusion(f32[160,4,2,20,1,1]{0,3,2,5,4,1:T(8,128)} %constant.163, f32[2,2,2,20,20]{3,4,1,2,0:T(8,128)S(1)} %copy.29), kind=kOutput, calls=%fused_computation.1 | convolution fusion | flops 24576000 | bytes 320000 | tf_op jit(solution)/shard_map/rqyf,zyxfn->zrnxq/dot_general | solution.py:87
  33.8 0.3 copy.30
  34.0 0.9 copy.32
  34.9 1.3 convolution_bitcast_fusion.3
  36.3 0.1 copy.61
  36.3 0.8 copy.31
  37.1 0.1 dynamic_slice.3
  37.2 0.1 concatenate.22.refs_0_
  37.3 1.8 %pad_maximum_fusion.1.mid_left = f32[3,160,160]{2,1,0:T(8,128)} fusion(f32[2,160,160]{2,1,0:T(8,128)} %copy.32, f32[1,160,160]{2,1,0:T(8,128)} %copy.31), kind=kLoop, calls=%fused_computation.6 | loop fusion | flops 76800 | bytes 614400 | tf_op jit(solution)/shard_map/concatenate | solution.py:88
  39.1 1.8 %pad_maximum_fusion.fine_left = f32[3,192,160]{2,1,0:T(8,128)} fusion(f32[2,192,160]{2,1,0:T(8,128)} %copy.39, f32[1,192,160]{2,1,0:T(8,128)S(1)} %copy-done.3), kind=kLoop, calls=%fused_computation.5 | loop fusion | flops 92160 | bytes 737280 | tf_op jit(solution)/shard_map/concatenate | solution.py:88
  41.0 43.0 %all-to-all-done.refs_1_ = f32[16,380,128]{2,1,0:T(8,128)S(1)} async-done(((f32[16,380,128]{2,1,0:T(8,128)}), f32[16,380,128]{2,1,0:T(8,128)S(1)}, u32[]{:S(2)}, u32[]{:S(2)}) %all-to-all-start) | async-done | bytes 3112992 | tf_op jit(solution)/shard_map/all_to_all | solution.py:345
  83.9 2.8 %coarse.1 = f32[24,2048]{1,0:T(8,128)S(1)} custom-call(s32[18]{0:T(128)S(1)} %concatenate.22.refs_0_, f32[16,380,128]{2,1,0:T(8,128)S(1)} %all-to-all-done.refs_1_, f32[24,216]{1,0:T(8,128)S(1)} %copy.43.refs_2_), custom_call_target="tpu_custom_call" | custom-call | tf_op jit(solution)/shard_map/coarse/pallas_call | solution.py:361
  86.8 0.1 reshape.109
  86.9 0.0 copy-start.1
  87.0 1.1 copy-done.1
  88.0 1.0 copy-done.2
  89.0 23.0 %fine.1 = (f32[16,128,512]{2,1,0:T(8,128)}, f32[8,128,512]{2,1,0:T(8,128)}, f32[16,64,512]{2,1,0:T(8,128)}, f32[128,512]{1,0:T(8,128)S(1)}, f32[8,16,512]{2,1,0:T(8,128)S(1)}) custom-call(s32[1]{0:T(128)} %bitcast.ints_ref, f32[3,160,160]{2,1,0:T(8,128)S(1)} %copy-done.2, f32[3,192,160]{2,1,0:T(8,128)S(1)} %copy-done.1, f32[20,2,16,128]{3,2,1,0:T(8,128)S(1)} %pad.13.upper, ...), custom_call_target="tpu_custom_call" | custom-call | tf_op jit(solution)/shard_map/fine/pallas_call | solution.py:375
  112.0 0.1 collective-permute-start.1
  112.1 13.8 %collective-permute-start = (f32[128,512]{1,0:T(8,128)S(1)}, f32[128,512]{1,0:T(8,128)S(1)}, u32[]{:S(2)}, u32[]{:S(2)}) collective-permute-start(f32[128,512]{1,0:T(8,128)S(1)} %get-tuple-element.34), channel_id=1, source_target_pairs={{2,0},{4,2},{6,4},{8,6},{10,8},{12,10},{14,12},{16,14},{18,16},{20... | collective-permute-start | bytes 786440 | tf_op jit(solution)/shard_map/ppermute | solution.py:415
  125.9 0.0 collective-permute-done.1
  125.9 1.0 reshape_add_fusion
  126.9 1.8 %scatter-add.9 = f32[16,64,512]{2,1,0:T(8,128)} dynamic-update-slice(f32[16,64,512]{2,1,0:T(8,128)} %get-tuple-element.35, f32[16,1,512]{2,1,0:T(1,128)S(1)} %reshape_add_fusion, s32[]{:T(128)} %constant.140.clone.1, s32[]{:T(128)} %constant.150.clone.1, s32[]{:T(128)} %constant.140.clone.1) | dynamic-update-slice | bytes 65540 | tf_op jit(solution)/shard_map/scatter-add | solution.py:419
  128.6 3.4 %collective-permute-done = f32[128,512]{1,0:T(8,128)S(1)} collective-permute-done((f32[128,512]{1,0:T(8,128)S(1)}, f32[128,512]{1,0:T(8,128)S(1)}, u32[]{:S(2)}, u32[]{:S(2)}) %collective-permute-start) | collective-permute-done | bytes 262176 | tf_op jit(solution)/shard_map/ppermute | solution.py:415
  132.1 1.7 %fusion = f32[8,128,512]{2,1,0:T(8,128)} fusion(f32[8,128,512]{2,1,0:T(8,128)} %get-tuple-element.33, f32[128,512]{1,0:T(8,128)S(1)} %collective-permute-done), kind=kLoop, calls=%fused_computation.8 | loop fusion | flops 65536 | bytes 786432 | tf_op jit(solution)/shard_map/scatter-add | solution.py:418
  (14 shorter events, 0.1 us)
Async XLA Ops:
  12.9 1.7 %copy-start = (f32[16,380,128]{2,1,0:T(8,128)}, f32[16,380,128]{2,1,0:T(8,128)S(1)}, u32[]{:S(2)}) copy-start(f32[16,380,128]{2,1,0:T(8,128)S(1)} %pack.1) | copy-start | bytes 9338884
  14.6 9.2 %copy-start.7 = (f32[20,20]{1,0:T(8,128)S(1)}, f32[20,20]{1,0:T(8,128)}, u32[]{:S(2)}) copy-start(f32[20,20]{1,0:T(8,128)} %param.19) | copy-start | bytes 4804
  14.6 9.9 %copy-start.4 = (f32[8,20,20]{2,0,1:T(8,128)S(1)}, f32[8,20,20]{2,0,1:T(8,128)}, u32[]{:S(2)}) copy-start(f32[8,20,20]{2,0,1:T(8,128)} %param.18) | copy-start | bytes 38404
  14.6 69.3 %all-to-all-start = ((f32[16,380,128]{2,1,0:T(8,128)}), f32[16,380,128]{2,1,0:T(8,128)S(1)}, u32[]{:S(2)}, u32[]{:S(2)}) async-start(f32[16,380,128]{2,1,0:T(8,128)} %copy-done), calls=%async_computation | async-start | bytes 6291456 | tf_op jit(solution)/shard_map/all_to_all | solution.py:345
  23.9 0.6 copy-start.6
  25.9 0.6 copy-start.5
  28.2 6.7 %copy-start.8 = (f32[20,20]{1,0:T(8,128)S(1)}, f32[20,20]{1,0:T(8,128)}, u32[]{:S(2)}) copy-start(f32[20,20]{1,0:T(8,128)} %param.19) | copy-start | bytes 4804
  30.4 6.7 %copy-start.9 = (s32[16]{0:T(128)S(1)}, s32[16]{0:T(128)}, u32[]{:S(2)}) copy-start(s32[16]{0:T(128)} %param.16) | copy-start | bytes 196
  34.9 4.2 %copy-start.3 = (f32[1,192,160]{2,1,0:T(8,128)S(1)}, f32[1,192,160]{2,1,0:T(8,128)}, u32[]{:S(2)}) copy-start(f32[1,192,160]{2,1,0:T(8,128)} %copy.38) | copy-start | bytes 368644
  86.9 1.1 copy-start.1
  88.0 1.0 copy-start.2
  112.0 13.8 %collective-permute-start.1 = (f32[16,512]{1,0:T(8,128)S(1)}, f32[16,512]{1,0:T(8,128)S(1)}, u32[]{:S(2)}, u32[]{:S(2)}) collective-permute-start(f32[16,512]{1,0:T(8,128)S(1)} %bitcast.92), channel_id=1, source_target_pairs={{1,0},{0,1},{3,2},{2,3},{5,4},{4,5},{7,6},{6,7},{9,8},{8,9},{11,10... | collective-permute-start | bytes 98312 | tf_op jit(solution)/shard_map/ppermute | solution.py:417
  112.1 19.9 %collective-permute-start = (f32[128,512]{1,0:T(8,128)S(1)}, f32[128,512]{1,0:T(8,128)S(1)}, u32[]{:S(2)}, u32[]{:S(2)}) collective-permute-start(f32[128,512]{1,0:T(8,128)S(1)} %get-tuple-element.34), channel_id=1, source_target_pairs={{2,0},{4,2},{6,4},{8,6},{10,8},{12,10},{14,12},{16,14},{18,16},{20... | collective-permute-start | bytes 786440 | tf_op jit(solution)/shard_map/ppermute | solution.py:415
